TPU v7x, 32 devices: a whole 2x2x4 slice. The times are simulated.
32 devices in a mesh: gx: 4 (over y, core), gy: 2 (over x), gz: 4 (over z).
Axes of the slice: x: 2, y: 2, z: 4, core: 2. Of those that a mesh axis runs over, the one named last changes fastest.
Arguments:
- old_basis: float32 [4, 32, 32, 512], P(None, 'gx', 'gy', 'gz'), may hold values from -4 to 4, as said below
- previous: float32 [4, 32, 32, 512], P(None, 'gx', 'gy', 'gz'), as said below
- incoming: float32 [4, 32, 32, 512], P(None, 'gx', 'gy', 'gz'), may hold values from -6 to 6
- coefficient: float32 [32, 32, 512], P('gx', 'gy', 'gz'), may hold values from 0.5 to 4
Outputs:
- orthonormal: float32 [4, 32, 32, 512], P(None, 'gx', 'gy', 'gz')
- projection: float32 [4, 4], replicated
- triangle: float32 [4, 4], replicated
- preconditioned: float32 [4, 32, 32, 512], P(None, 'gx', 'gy', 'gz')
- operated: float32 [4, 32, 32, 512], P(None, 'gx', 'gy', 'gz')
Inputs may be any that keep to these rules, and one draw needn't show every extreme that they name: `old_basis`: entries of order one; the basis vectors are independent, so every Gram matrix formed from them is well conditioned. `previous`: entries of order one; each vector has a part outside the span of old_basis of norm of order one under the inner product.
All inputs are finite; a program needn't handle non-finite values.
Results may differ from a plain program's by a relative error of at most 0.0003.
Values sent between devices are 32-bit elements; how exact they have to be, the bound alone decides.
No kernel may reach another device: no remote copies, remote signals or barrier semaphores. Data moves between devices by JAX's collectives and lax.ppermute only.
A program may use at most 64 MiB of HBM per device.

v0:
```python
import jax
import jax.numpy as jnp
from jax import lax
from jax.sharding import PartitionSpec as P

LEVELS = 6
COARSE_SWEEPS = 4
OMEGA = 0.8
HIGH = lax.Precision.HIGHEST


def with_halo(shard, sides, width):
    for axis, dim in sides:
        count, length = (lax.axis_size(axis), shard.shape[dim])
        up = [(i, (i + 1) % count) for i in range(count - 1)]
        down = [(j, i) for i, j in up]
        last = lax.slice_in_dim(shard, length - width, length, axis=dim)
        leading = lax.slice_in_dim(shard, 0, width, axis=dim)
        before = lax.ppermute(last, axis, up)
        after = lax.ppermute(leading, axis, down)
        shard = jnp.concatenate([before, shard, after], axis=dim)
    return shard


def stencil(extended, coeffs, factor):
    center = extended[:, 1:-1, 1:-1, 1:-1]
    total = extended[:, 2:, 1:-1, 1:-1] + extended[:, :-2, 1:-1, 1:-1]
    total = total + extended[:, 1:-1, 2:, 1:-1] + extended[:, 1:-1, :-2, 1:-1]
    total = total + extended[:, 1:-1, 1:-1, 2:] + extended[:, 1:-1, 1:-1, :-2]
    return factor * coeffs * (6.0 * center - total)


def zero_margin(field):
    return jnp.pad(field, ((0, 0), (1, 1), (1, 1), (1, 1)))


def with_faces(field):
    return with_halo(field, (("gx", 1), ("gy", 2), ("gz", 3)), 1)


def restrict(field):
    depth, size_a, size_b, size_c = field.shape
    return field.reshape(depth, size_a // 2, 2, size_b // 2, 2, size_c // 2, 2).mean(axis=(2, 4, 6))


def prolong(field):
    return jnp.repeat(jnp.repeat(jnp.repeat(field, 2, axis=1), 2, axis=2), 2, axis=3)


def whole_cycle(source, coeff_list, level):
    coeffs = coeff_list[level]
    factor = 0.25**level
    diagonal = 6.0 * factor * coeffs
    iterate = OMEGA * source / diagonal
    if level == LEVELS - 1:
        for sweep in range(COARSE_SWEEPS - 1):
            iterate = (
                iterate
                + OMEGA * (source - stencil(zero_margin(iterate), coeffs, factor)) / diagonal
            )
        return iterate
    iterate = iterate + OMEGA * (source - stencil(zero_margin(iterate), coeffs, factor)) / diagonal
    residue = source - stencil(zero_margin(iterate), coeffs, factor)
    iterate = iterate + prolong(whole_cycle(restrict(residue), coeff_list, level + 1))
    iterate = iterate + OMEGA * (source - stencil(zero_margin(iterate), coeffs, factor)) / diagonal
    return iterate


def agglomerate(source, coeffs, start_level):
    vectors = source.shape[0]
    stacked = jnp.concatenate([source, coeffs[None]], axis=0)
    depth, size_a, size_b, size_c = stacked.shape
    flattened = stacked.reshape(depth, size_a * size_b * size_c)
    gathered = lax.all_gather(flattened, ("gx", "gy", "gz"), axis=1, tiled=True)
    count_x, count_y, count_z = (lax.axis_size("gx"), lax.axis_size("gy"), lax.axis_size("gz"))
    gathered = gathered.reshape(depth, count_x, count_y, count_z, size_a, size_b, size_c)
    gathered = gathered.transpose(0, 1, 4, 2, 5, 3, 6).reshape(
        depth, count_x * size_a, count_y * size_b, count_z * size_c
    )
    coarse_list = [gathered[vectors]]
    for level in range(LEVELS - 1 - start_level):
        coarse_list.append(restrict(coarse_list[-1][None])[0])
    solution = whole_cycle(gathered[:vectors], [None] * start_level + coarse_list, start_level)
    starts = (
        jnp.zeros((), jnp.int32),
        lax.axis_index("gx") * size_a,
        lax.axis_index("gy") * size_b,
        lax.axis_index("gz") * size_c,
    )
    return lax.dynamic_slice(solution, starts, (vectors, size_a, size_b, size_c))


def local_cycle(source, coeff_list, level, start_level):
    coeffs = coeff_list[level]
    if level == start_level:
        return agglomerate(source, coeffs, start_level)
    factor = 0.25**level
    diagonal = 6.0 * factor * coeffs
    vectors = source.shape[0]
    stacked = jnp.concatenate([source, coeffs[None]], axis=0)
    widened = with_halo(stacked, (("gx", 1), ("gy", 2), ("gz", 3)), 2)
    source_wide = widened[:vectors]
    coeff_wide = widened[vectors]
    safe_wide = jnp.where(coeff_wide > 0.0, coeff_wide, 1.0)
    sweep_one = OMEGA * source_wide / (6.0 * factor * safe_wide)
    inner_coeff = coeff_wide[1:-1, 1:-1, 1:-1]
    inner_safe = safe_wide[1:-1, 1:-1, 1:-1]
    sweep_two = sweep_one[:, 1:-1, 1:-1, 1:-1] + OMEGA * (
        source_wide[:, 1:-1, 1:-1, 1:-1] - stencil(sweep_one, inner_coeff, factor)
    ) / (6.0 * factor * inner_safe)
    iterate = sweep_two[:, 1:-1, 1:-1, 1:-1]
    residue = source - stencil(sweep_two, coeffs, factor)
    iterate = iterate + prolong(local_cycle(restrict(residue), coeff_list, level + 1, start_level))
    iterate = iterate + OMEGA * (source - stencil(with_faces(iterate), coeffs, factor)) / diagonal
    return iterate


def triangular_inverse(lower):
    order = lower.shape[0]
    identity = jnp.eye(order, dtype=lower.dtype)
    inverse = jnp.zeros_like(lower)
    for row in range(order):
        values = identity[row] - jnp.dot(lower[row, :row], inverse[:row], precision=HIGH)
        inverse = inverse.at[row].set(values / lower[row, row])
    return inverse


def per_device(old_basis, previous, incoming, coefficient):
    local_cells = old_basis.shape[1] * old_basis.shape[2] * old_basis.shape[3]
    total_cells = float(
        local_cells * lax.axis_size("gx") * lax.axis_size("gy") * lax.axis_size("gz")
    )
    basis_local = jnp.einsum("mxyz,jxyz->mj", old_basis, previous, precision=HIGH)
    projection = lax.psum(basis_local, ("gx", "gy", "gz")) / total_cells
    remainder = previous - jnp.einsum("mxyz,mj->jxyz", old_basis, projection, precision=HIGH)
    gram_local = jnp.einsum("ixyz,jxyz->ij", remainder, remainder, precision=HIGH)
    gram = lax.psum(gram_local, ("gx", "gy", "gz")) / total_cells
    start_level = LEVELS - 3
    coeff_list = [coefficient]
    for level in range(start_level):
        coeff_list.append(restrict(coeff_list[-1][None])[0])
    preconditioned = local_cycle(incoming, coeff_list, 0, start_level)
    operated = stencil(with_faces(preconditioned), coefficient, 1.0)
    lower = jnp.linalg.cholesky(gram)
    inverse = triangular_inverse(lower)
    orthonormal = jnp.einsum("ji,ixyz->jxyz", inverse, remainder, precision=HIGH)
    return (orthonormal, projection, lower.T, preconditioned, operated)


def solution(mesh):
    in_specs = (
        P(None, "gx", "gy", "gz"),
        P(None, "gx", "gy", "gz"),
        P(None, "gx", "gy", "gz"),
        P("gx", "gy", "gz"),
    )
    out_specs = (
        P(None, "gx", "gy", "gz"),
        P(),
        P(),
        P(None, "gx", "gy", "gz"),
        P(None, "gx", "gy", "gz"),
    )
    return jax.shard_map(
        per_device, mesh=mesh, in_specs=in_specs, out_specs=out_specs, check_vma=False
    )
```

profile of v0, /device:TPU:25, one launch (start us, length us, event | category | flops | bytes accessed | tf_op | source)
XLA Modules:
  0.0 369.9 jit_solution(2257460580880497571)
XLA Ops:
  1.6 3.7 %collective-permute-start = (f32[5,2,16,128]{3,2,1,0:T(8,128)S(1)}, f32[5,2,16,128]{3,2,1,0:T(8,128)S(1)}, u32[]{:S(2)}, u32[]{:S(2)}) collective-permute-start(f32[5,2,16,128]{3,2,1,0:T(8,128)S(1)} %get-tuple-element.122), channel_id=1, source_target_pairs={{0,8},{8,16},{16,24},{1,9},{9,17},{17,25},{2,10},{10,18},{18,26},{... | collective-permute-start | bytes 245768 | tf_op jit(solution)/shard_map/ppermute | solution.py:19
  7.3 3.8 %collective-permute-done.1 = f32[5,2,16,128]{3,2,1,0:T(8,128)S(1)} collective-permute-done((f32[5,2,16,128]{3,2,1,0:T(8,128)S(1)}, f32[5,2,16,128]{3,2,1,0:T(8,128)S(1)}, u32[]{:S(2)}, u32[]{:S(2)}) %collective-permute-start.1) | collective-permute-done | bytes 81952 | tf_op jit(solution)/shard_map/ppermute | solution.py:20
  19.0 5.5 %reshape_broadcast_in_dim.3 = f32[4,2,8,2,64,2]{5,4,3,2,1,0:T(8,128)} reshape(f32[8,16,128]{2,1,0:T(8,128)S(1)} %copy-done.1) | data formatting | bytes 131072 | tf_op jit(solution)/shard_map/reshape;broadcast_in_dim | solution.py:43
  29.8 4.0 %collective-permute-start.5 = (f32[5,12,20,2]{2,3,1,0:T(2,128)S(1)}, f32[5,12,20,2]{2,3,1,0:T(2,128)S(1)}, u32[]{:S(2)}, u32[]{:S(2)}) collective-permute-start(f32[5,12,20,2]{2,3,1,0:T(2,128)S(1)} %copy.767), channel_id=1, source_target_pairs={{1,0},{2,1},{3,2},{5,4},{6,5},{7,6},{9,8},{10,9},{11,10},{13,12},{... | collective-permute-start | bytes 28808 | tf_op jit(solution)/shard_map/ppermute | solution.py:20
  33.8 38.6 %psum.14 = f32[4,4]{0,1:T(4,128)S(1)} all-reduce(f32[4,4]{0,1:T(4,128)S(1)} %convolution_bitcast_fusion.1), channel_id=1, replica_groups=mesh['gx'=4,'gy'=2,'gz'=4] {'gx','gy','gz'}, use_global_device_ids=true, to_apply=%region_0.0 | all-reduce | flops 16 | bytes 128 | tf_op jit(solution)/shard_map/psum | solution.py:134
  77.0 4.7 %copy.690 = f32[4,8,16,128]{0,3,2,1:T(8,128)} copy(f32[4,8,16,128]{3,2,1,0:T(8,128)S(1)} %fusion.35) | data formatting | bytes 524288 | tf_op jit(solution)/shard_map/sub | solution.py:112
  81.7 8.7 %reduce_sum.102 = f32[4,4,8,64]{0,3,2,1:T(8,128)S(1)} reduce(f32[4,4,2,8,2,64,2]{0,6,5,4,3,2,1:T(2,128)} %bitcast.130, f32[]{:T(128)} %constant.248.clone.1), dimensions={2,4,6}, to_apply=%region_4.0 | reduce | flops 57344 | bytes 294916 | tf_op jit(solution)/shard_map/reduce_sum | solution.py:43
  90.8 5.3 %collective-permute-start.6 = (f32[5,2,8,64]{3,2,1,0:T(8,128)S(1)}, f32[5,2,8,64]{3,2,1,0:T(8,128)S(1)}, u32[]{:S(2)}, u32[]{:S(2)}) collective-permute-start(f32[5,2,8,64]{3,2,1,0:T(8,128)S(1)} %get-tuple-element.154), channel_id=1, source_target_pairs={{0,8},{8,16},{16,24},{1,9},{9,17},{17,25},{2,10},{10,18},{18,26},{... | collective-permute-start | bytes 61448 | tf_op jit(solution)/shard_map/ppermute | solution.py:19
  109.4 4.0 %collective-permute-start.11 = (f32[5,8,12,2]{3,1,2,0:T(8,128)S(1)}, f32[5,8,12,2]{3,1,2,0:T(8,128)S(1)}, u32[]{:S(2)}, u32[]{:S(2)}) collective-permute-start(f32[5,8,12,2]{3,1,2,0:T(8,128)S(1)} %get-tuple-element.131), channel_id=1, source_target_pairs={{1,0},{2,1},{3,2},{5,4},{6,5},{7,6},{9,8},{10,9},{11,10},{13,12},{... | collective-permute-start | bytes 11528 | tf_op jit(solution)/shard_map/ppermute | solution.py:20
  126.0 38.6 %psum.15 = f32[4,4]{0,1:T(4,128)S(1)} all-reduce(f32[4,4]{0,1:T(4,128)S(1)} %convolution_bitcast_fusion), channel_id=1, replica_groups=mesh['gx'=4,'gy'=2,'gz'=4] {'gx','gy','gz'}, use_global_device_ids=true, to_apply=%region_1.0 | all-reduce | flops 16 | bytes 128 | tf_op jit(solution)/shard_map/psum | solution.py:137
  164.7 4.3 %collective-permute-start.14 = (f32[5,6,2,32]{3,2,1,0:T(2,128)S(1)}, f32[5,6,2,32]{3,2,1,0:T(2,128)S(1)}, u32[]{:S(2)}, u32[]{:S(2)}) collective-permute-start(f32[5,6,2,32]{3,2,1,0:T(2,128)S(1)} %get-tuple-element.158), channel_id=1, source_target_pairs={{0,4},{1,5},{2,6},{3,7},{8,12},{9,13},{10,14},{11,15},{16,20},{17,... | collective-permute-start | bytes 23048 | tf_op jit(solution)/shard_map/ppermute | solution.py:19
  175.1 4.0 %collective-permute-start.17 = (f32[5,6,8,2]{3,2,1,0:T(8,128)S(1)}, f32[5,6,8,2]{3,2,1,0:T(8,128)S(1)}, u32[]{:S(2)}, u32[]{:S(2)}) collective-permute-start(f32[5,6,8,2]{3,2,1,0:T(8,128)S(1)} %get-tuple-element.151), channel_id=1, source_target_pairs={{1,0},{2,1},{3,2},{5,4},{6,5},{7,6},{9,8},{10,9},{11,10},{13,12},{... | collective-permute-start | bytes 5768 | tf_op jit(solution)/shard_map/ppermute | solution.py:20
  181.9 61.1 %all-gather = f32[32,32,5]{1,2,0:T(8,128)S(1)} all-gather(f32[1,32,5]{1,2,0:T(8,128)S(1)} %maximum_bitcast_fusion), channel_id=1, replica_groups=mesh['gx'=4,'gy'=2,'gz'=4] {'gx','gy','gz'}, dimensions={0}, use_global_device_ids=true | all-gather | bytes 21120 | tf_op jit(solution)/shard_map/all_gather | solution.py:74
  247.3 8.6 %collective-permute-start.18 = (f32[4,1,4,32]{3,2,1,0:T(4,128)S(1)}, f32[4,1,4,32]{3,2,1,0:T(4,128)S(1)}, u32[]{:S(2)}, u32[]{:S(2)}) collective-permute-start(f32[4,1,4,32]{3,2,1,0:T(4,128)S(1)} %get-tuple-element.175), channel_id=1, source_target_pairs={{8,0},{16,8},{24,16},{9,1},{17,9},{25,17},{10,2},{18,10},{26,18},{... | collective-permute-start | bytes 6152 | tf_op jit(solution)/shard_map/ppermute | solution.py:20
  271.7 4.3 %collective-permute-done.23 = f32[4,4,6,1]{3,1,2,0:T(4,128)S(1)} collective-permute-done((f32[4,4,6,1]{3,1,2,0:T(4,128)S(1)}, f32[4,4,6,1]{3,1,2,0:T(4,128)S(1)}, u32[]{:S(2)}, u32[]{:S(2)}) %collective-permute-start.23) | collective-permute-done | bytes 416 | tf_op jit(solution)/shard_map/ppermute | solution.py:19
  279.6 5.3 %collective-permute-start.25 = (f32[4,1,8,64]{3,2,1,0:T(8,128)S(1)}, f32[4,1,8,64]{3,2,1,0:T(8,128)S(1)}, u32[]{:S(2)}, u32[]{:S(2)}) collective-permute-start(f32[4,1,8,64]{3,2,1,0:T(8,128)S(1)} %get-tuple-element.156), channel_id=1, source_target_pairs={{0,8},{8,16},{16,24},{1,9},{9,17},{17,25},{2,10},{10,18},{18,26},{... | collective-permute-start | bytes 24584 | tf_op jit(solution)/shard_map/ppermute | solution.py:19
  292.4 3.7 %collective-permute-start.28 = (f32[4,6,10,1]{3,0,2,1:T(4,128)S(1)}, f32[4,6,10,1]{3,0,2,1:T(4,128)S(1)}, u32[]{:S(2)}, u32[]{:S(2)}) collective-permute-start(f32[4,6,10,1]{3,0,2,1:T(4,128)S(1)} %get-tuple-element.146), channel_id=1, source_target_pairs={{1,0},{2,1},{3,2},{5,4},{6,5},{7,6},{9,8},{10,9},{11,10},{13,12},{... | collective-permute-start | bytes 2888 | tf_op jit(solution)/shard_map/ppermute | solution.py:20
  298.2 4.1 %collective-permute-done.29 = f32[4,6,10,1]{3,0,2,1:T(4,128)S(1)} collective-permute-done((f32[4,6,10,1]{3,0,2,1:T(4,128)S(1)}, f32[4,6,10,1]{3,0,2,1:T(4,128)S(1)}, u32[]{:S(2)}, u32[]{:S(2)}) %collective-permute-start.29) | collective-permute-done | bytes 992 | tf_op jit(solution)/shard_map/ppermute | solution.py:19
  309.8 6.7 %collective-permute-start.31 = (f32[4,1,16,128]{3,2,1,0:T(8,128)S(1)}, f32[4,1,16,128]{3,2,1,0:T(8,128)S(1)}, u32[]{:S(2)}, u32[]{:S(2)}) collective-permute-start(f32[4,1,16,128]{3,2,1,0:T(8,128)S(1)} %get-tuple-element.128), channel_id=1, source_target_pairs={{0,8},{8,16},{16,24},{1,9},{9,17},{17,25},{2,10},{10,18},{18,26},{... | collective-permute-start | bytes 98312 | tf_op jit(solution)/shard_map/ppermute | solution.py:19
  331.4 4.0 %collective-permute-done.34 = f32[4,10,18,1]{3,0,2,1:T(4,128)S(1)} collective-permute-done((f32[4,10,18,1]{3,0,2,1:T(4,128)S(1)}, f32[4,10,18,1]{3,0,2,1:T(4,128)S(1)}, u32[]{:S(2)}, u32[]{:S(2)}) %collective-permute-start.34) | collective-permute-done | bytes 2912 | tf_op jit(solution)/shard_map/ppermute | solution.py:20
  335.4 4.1 %collective-permute-done.35 = f32[4,10,18,1]{3,0,2,1:T(4,128)S(1)} collective-permute-done((f32[4,10,18,1]{3,0,2,1:T(4,128)S(1)}, f32[4,10,18,1]{3,0,2,1:T(4,128)S(1)}, u32[]{:S(2)}, u32[]{:S(2)}) %collective-permute-start.35) | collective-permute-done | bytes 2912 | tf_op jit(solution)/shard_map/ppermute | solution.py:19
  342.1 4.1 %collective-permute-start.37 = (f32[4,1,16,128]{3,2,1,0:T(8,128)S(1)}, f32[4,1,16,128]{3,2,1,0:T(8,128)S(1)}, u32[]{:S(2)}, u32[]{:S(2)}) collective-permute-start(f32[4,1,16,128]{3,2,1,0:T(8,128)S(1)} %get-tuple-element.126), channel_id=1, source_target_pairs={{0,8},{8,16},{16,24},{1,9},{9,17},{17,25},{2,10},{10,18},{18,26},{... | collective-permute-start | bytes 98312 | tf_op jit(solution)/shard_map/ppermute | solution.py:19
  359.5 4.7 %collective-permute-done.40 = f32[4,10,18,1]{3,0,2,1:T(4,128)S(1)} collective-permute-done((f32[4,10,18,1]{3,0,2,1:T(4,128)S(1)}, f32[4,10,18,1]{3,0,2,1:T(4,128)S(1)}, u32[]{:S(2)}, u32[]{:S(2)}) %collective-permute-start.40) | collective-permute-done | bytes 2912 | tf_op jit(solution)/shard_map/ppermute | solution.py:20
  364.2 4.4 %collective-permute-done.41 = f32[4,10,18,1]{3,0,2,1:T(4,128)S(1)} collective-permute-done((f32[4,10,18,1]{3,0,2,1:T(4,128)S(1)}, f32[4,10,18,1]{3,0,2,1:T(4,128)S(1)}, u32[]{:S(2)}, u32[]{:S(2)}) %collective-permute-start.41) | collective-permute-done | bytes 2912 | tf_op jit(solution)/shard_map/ppermute | solution.py:19
  (279 shorter events, 127.5 us)
Async XLA Ops:
  12.1 15.0 %collective-permute-start.2 = (f32[5,12,2,128]{3,2,1,0:T(2,128)S(1)}, f32[5,12,2,128]{3,2,1,0:T(2,128)S(1)}, u32[]{:S(2)}, u32[]{:S(2)}) collective-permute-start(f32[5,12,2,128]{3,2,1,0:T(2,128)S(1)} %get-tuple-element.108), channel_id=1, source_target_pairs={{0,4},{1,5},{2,6},{3,7},{8,12},{9,13},{10,14},{11,15},{16,20},{17,... | collective-permute-start | bytes 184328 | tf_op jit(solution)/shard_map/ppermute | solution.py:19
  15.3 11.9 %collective-permute-start.3 = (f32[5,12,2,128]{3,2,1,0:T(2,128)S(1)}, f32[5,12,2,128]{3,2,1,0:T(2,128)S(1)}, u32[]{:S(2)}, u32[]{:S(2)}) collective-permute-start(f32[5,12,2,128]{3,2,1,0:T(2,128)S(1)} %get-tuple-element.109), channel_id=1, source_target_pairs={{4,0},{5,1},{6,2},{7,3},{12,8},{13,9},{14,10},{15,11},{20,16},{21,... | collective-permute-start | bytes 184328 | tf_op jit(solution)/shard_map/ppermute | solution.py:20
  28.0 44.4 %collective-permute-start.4 = (f32[5,12,20,2]{2,3,1,0:T(2,128)S(1)}, f32[5,12,20,2]{2,3,1,0:T(2,128)S(1)}, u32[]{:S(2)}, u32[]{:S(2)}) collective-permute-start(f32[5,12,20,2]{2,3,1,0:T(2,128)S(1)} %copy.766), channel_id=1, source_target_pairs={{0,1},{1,2},{2,3},{4,5},{5,6},{6,7},{8,9},{9,10},{10,11},{12,13},{... | collective-permute-start | bytes 28808 | tf_op jit(solution)/shard_map/ppermute | solution.py:19
  29.8 43.1 %collective-permute-start.5 = (f32[5,12,20,2]{2,3,1,0:T(2,128)S(1)}, f32[5,12,20,2]{2,3,1,0:T(2,128)S(1)}, u32[]{:S(2)}, u32[]{:S(2)}) collective-permute-start(f32[5,12,20,2]{2,3,1,0:T(2,128)S(1)} %copy.767), channel_id=1, source_target_pairs={{1,0},{2,1},{3,2},{5,4},{6,5},{7,6},{9,8},{10,9},{11,10},{13,12},{... | collective-permute-start | bytes 28808 | tf_op jit(solution)/shard_map/ppermute | solution.py:20
  90.8 8.9 %collective-permute-start.6 = (f32[5,2,8,64]{3,2,1,0:T(8,128)S(1)}, f32[5,2,8,64]{3,2,1,0:T(8,128)S(1)}, u32[]{:S(2)}, u32[]{:S(2)}) collective-permute-start(f32[5,2,8,64]{3,2,1,0:T(8,128)S(1)} %get-tuple-element.154), channel_id=1, source_target_pairs={{0,8},{8,16},{16,24},{1,9},{9,17},{17,25},{2,10},{10,18},{18,26},{... | collective-permute-start | bytes 61448 | tf_op jit(solution)/shard_map/ppermute | solution.py:19
  108.1 9.3 %collective-permute-start.10 = (f32[5,8,12,2]{3,1,2,0:T(8,128)S(1)}, f32[5,8,12,2]{3,1,2,0:T(8,128)S(1)}, u32[]{:S(2)}, u32[]{:S(2)}) collective-permute-start(f32[5,8,12,2]{3,1,2,0:T(8,128)S(1)} %get-tuple-element.130), channel_id=1, source_target_pairs={{0,1},{1,2},{2,3},{4,5},{5,6},{6,7},{8,9},{9,10},{10,11},{12,13},{... | collective-permute-start | bytes 11528 | tf_op jit(solution)/shard_map/ppermute | solution.py:19
  109.4 9.7 %collective-permute-start.11 = (f32[5,8,12,2]{3,1,2,0:T(8,128)S(1)}, f32[5,8,12,2]{3,1,2,0:T(8,128)S(1)}, u32[]{:S(2)}, u32[]{:S(2)}) collective-permute-start(f32[5,8,12,2]{3,1,2,0:T(8,128)S(1)} %get-tuple-element.131), channel_id=1, source_target_pairs={{1,0},{2,1},{3,2},{5,4},{6,5},{7,6},{9,8},{10,9},{11,10},{13,12},{... | collective-permute-start | bytes 11528 | tf_op jit(solution)/shard_map/ppermute | solution.py:20
  121.7 42.9 %collective-permute-start.12 = (f32[5,2,4,32]{3,2,1,0:T(4,128)S(1)}, f32[5,2,4,32]{3,2,1,0:T(4,128)S(1)}, u32[]{:S(2)}, u32[]{:S(2)}) collective-permute-start(f32[5,2,4,32]{3,2,1,0:T(4,128)S(1)} %pad_maximum_fusion.50), channel_id=1, source_target_pairs={{0,8},{8,16},{16,24},{1,9},{9,17},{17,25},{2,10},{10,18},{18,26},{... | collective-permute-start | bytes 15368 | tf_op jit(solution)/shard_map/ppermute | solution.py:19
  123.6 41.0 %collective-permute-start.13 = (f32[5,2,4,32]{3,2,1,0:T(4,128)S(1)}, f32[5,2,4,32]{3,2,1,0:T(4,128)S(1)}, u32[]{:S(2)}, u32[]{:S(2)}) collective-permute-start(f32[5,2,4,32]{3,2,1,0:T(4,128)S(1)} %pad_maximum_fusion.50), channel_id=1, source_target_pairs={{8,0},{16,8},{24,16},{9,1},{17,9},{25,17},{10,2},{18,10},{26,18},{... | collective-permute-start | bytes 15368 | tf_op jit(solution)/shard_map/ppermute | solution.py:20
  164.7 5.8 %collective-permute-start.14 = (f32[5,6,2,32]{3,2,1,0:T(2,128)S(1)}, f32[5,6,2,32]{3,2,1,0:T(2,128)S(1)}, u32[]{:S(2)}, u32[]{:S(2)}) collective-permute-start(f32[5,6,2,32]{3,2,1,0:T(2,128)S(1)} %get-tuple-element.158), channel_id=1, source_target_pairs={{0,4},{1,5},{2,6},{3,7},{8,12},{9,13},{10,14},{11,15},{16,20},{17,... | collective-permute-start | bytes 23048 | tf_op jit(solution)/shard_map/ppermute | solution.py:19
  175.1 5.8 %collective-permute-start.17 = (f32[5,6,8,2]{3,2,1,0:T(8,128)S(1)}, f32[5,6,8,2]{3,2,1,0:T(8,128)S(1)}, u32[]{:S(2)}, u32[]{:S(2)}) collective-permute-start(f32[5,6,8,2]{3,2,1,0:T(8,128)S(1)} %get-tuple-element.151), channel_id=1, source_target_pairs={{1,0},{2,1},{3,2},{5,4},{6,5},{7,6},{9,8},{10,9},{11,10},{13,12},{... | collective-permute-start | bytes 5768 | tf_op jit(solution)/shard_map/ppermute | solution.py:20
  247.3 12.6 %collective-permute-start.18 = (f32[4,1,4,32]{3,2,1,0:T(4,128)S(1)}, f32[4,1,4,32]{3,2,1,0:T(4,128)S(1)}, u32[]{:S(2)}, u32[]{:S(2)}) collective-permute-start(f32[4,1,4,32]{3,2,1,0:T(4,128)S(1)} %get-tuple-element.175), channel_id=1, source_target_pairs={{8,0},{16,8},{24,16},{9,1},{17,9},{25,17},{10,2},{18,10},{26,18},{... | collective-permute-start | bytes 6152 | tf_op jit(solution)/shard_map/ppermute | solution.py:20
  269.7 6.2 %collective-permute-start.23 = (f32[4,4,6,1]{3,1,2,0:T(4,128)S(1)}, f32[4,4,6,1]{3,1,2,0:T(4,128)S(1)}, u32[]{:S(2)}, u32[]{:S(2)}) collective-permute-start(f32[4,4,6,1]{3,1,2,0:T(4,128)S(1)} %get-tuple-element.163), channel_id=1, source_target_pairs={{0,1},{1,2},{2,3},{4,5},{5,6},{6,7},{8,9},{9,10},{10,11},{12,13},{... | collective-permute-start | bytes 1160 | tf_op jit(solution)/shard_map/ppermute | solution.py:19
  276.8 8.8 %collective-permute-start.24 = (f32[4,1,8,64]{3,2,1,0:T(8,128)S(1)}, f32[4,1,8,64]{3,2,1,0:T(8,128)S(1)}, u32[]{:S(2)}, u32[]{:S(2)}) collective-permute-start(f32[4,1,8,64]{3,2,1,0:T(8,128)S(1)} %get-tuple-element.157), channel_id=1, source_target_pairs={{8,0},{16,8},{24,16},{9,1},{17,9},{25,17},{10,2},{18,10},{26,18},{... | collective-permute-start | bytes 24584 | tf_op jit(solution)/shard_map/ppermute | solution.py:20
  279.6 6.1 %collective-permute-start.25 = (f32[4,1,8,64]{3,2,1,0:T(8,128)S(1)}, f32[4,1,8,64]{3,2,1,0:T(8,128)S(1)}, u32[]{:S(2)}, u32[]{:S(2)}) collective-permute-start(f32[4,1,8,64]{3,2,1,0:T(8,128)S(1)} %get-tuple-element.156), channel_id=1, source_target_pairs={{0,8},{8,16},{16,24},{1,9},{9,17},{17,25},{2,10},{10,18},{18,26},{... | collective-permute-start | bytes 24584 | tf_op jit(solution)/shard_map/ppermute | solution.py:19
  292.4 5.8 %collective-permute-start.28 = (f32[4,6,10,1]{3,0,2,1:T(4,128)S(1)}, f32[4,6,10,1]{3,0,2,1:T(4,128)S(1)}, u32[]{:S(2)}, u32[]{:S(2)}) collective-permute-start(f32[4,6,10,1]{3,0,2,1:T(4,128)S(1)} %get-tuple-element.146), channel_id=1, source_target_pairs={{1,0},{2,1},{3,2},{5,4},{6,5},{7,6},{9,8},{10,9},{11,10},{13,12},{... | collective-permute-start | bytes 2888 | tf_op jit(solution)/shard_map/ppermute | solution.py:20
  296.1 6.2 %collective-permute-start.29 = (f32[4,6,10,1]{3,0,2,1:T(4,128)S(1)}, f32[4,6,10,1]{3,0,2,1:T(4,128)S(1)}, u32[]{:S(2)}, u32[]{:S(2)}) collective-permute-start(f32[4,6,10,1]{3,0,2,1:T(4,128)S(1)} %get-tuple-element.147), channel_id=1, source_target_pairs={{0,1},{1,2},{2,3},{4,5},{5,6},{6,7},{8,9},{9,10},{10,11},{12,13},{... | collective-permute-start | bytes 2888 | tf_op jit(solution)/shard_map/ppermute | solution.py:19
  307.8 10.6 %collective-permute-start.30 = (f32[4,1,16,128]{3,2,1,0:T(8,128)S(1)}, f32[4,1,16,128]{3,2,1,0:T(8,128)S(1)}, u32[]{:S(2)}, u32[]{:S(2)}) collective-permute-start(f32[4,1,16,128]{3,2,1,0:T(8,128)S(1)} %get-tuple-element.129), channel_id=1, source_target_pairs={{8,0},{16,8},{24,16},{9,1},{17,9},{25,17},{10,2},{18,10},{26,18},{... | collective-permute-start | bytes 98312 | tf_op jit(solution)/shard_map/ppermute | solution.py:20
  309.8 8.7 %collective-permute-start.31 = (f32[4,1,16,128]{3,2,1,0:T(8,128)S(1)}, f32[4,1,16,128]{3,2,1,0:T(8,128)S(1)}, u32[]{:S(2)}, u32[]{:S(2)}) collective-permute-start(f32[4,1,16,128]{3,2,1,0:T(8,128)S(1)} %get-tuple-element.128), channel_id=1, source_target_pairs={{0,8},{8,16},{16,24},{1,9},{9,17},{17,25},{2,10},{10,18},{18,26},{... | collective-permute-start | bytes 98312 | tf_op jit(solution)/shard_map/ppermute | solution.py:19
  325.5 9.9 %collective-permute-start.34 = (f32[4,10,18,1]{3,0,2,1:T(4,128)S(1)}, f32[4,10,18,1]{3,0,2,1:T(4,128)S(1)}, u32[]{:S(2)}, u32[]{:S(2)}) collective-permute-start(f32[4,10,18,1]{3,0,2,1:T(4,128)S(1)} %get-tuple-element.116), channel_id=1, source_target_pairs={{1,0},{2,1},{3,2},{5,4},{6,5},{7,6},{9,8},{10,9},{11,10},{13,12},{... | collective-permute-start | bytes 8648 | tf_op jit(solution)/shard_map/ppermute | solution.py:20
  329.2 10.3 %collective-permute-start.35 = (f32[4,10,18,1]{3,0,2,1:T(4,128)S(1)}, f32[4,10,18,1]{3,0,2,1:T(4,128)S(1)}, u32[]{:S(2)}, u32[]{:S(2)}) collective-permute-start(f32[4,10,18,1]{3,0,2,1:T(4,128)S(1)} %get-tuple-element.117), channel_id=1, source_target_pairs={{0,1},{1,2},{2,3},{4,5},{5,6},{6,7},{8,9},{9,10},{10,11},{12,13},{... | collective-permute-start | bytes 8648 | tf_op jit(solution)/shard_map/ppermute | solution.py:19
  340.2 6.6 %collective-permute-start.36 = (f32[4,1,16,128]{3,2,1,0:T(8,128)S(1)}, f32[4,1,16,128]{3,2,1,0:T(8,128)S(1)}, u32[]{:S(2)}, u32[]{:S(2)}) collective-permute-start(f32[4,1,16,128]{3,2,1,0:T(8,128)S(1)} %get-tuple-element.127), channel_id=1, source_target_pairs={{8,0},{16,8},{24,16},{9,1},{17,9},{25,17},{10,2},{18,10},{26,18},{... | collective-permute-start | bytes 98312 | tf_op jit(solution)/shard_map/ppermute | solution.py:20
  354.2 10.0 %collective-permute-start.40 = (f32[4,10,18,1]{3,0,2,1:T(4,128)S(1)}, f32[4,10,18,1]{3,0,2,1:T(4,128)S(1)}, u32[]{:S(2)}, u32[]{:S(2)}) collective-permute-start(f32[4,10,18,1]{3,0,2,1:T(4,128)S(1)} %get-tuple-element.112), channel_id=1, source_target_pairs={{1,0},{2,1},{3,2},{5,4},{6,5},{7,6},{9,8},{10,9},{11,10},{13,12},{... | collective-permute-start | bytes 8648 | tf_op jit(solution)/shard_map/ppermute | solution.py:20
  356.1 12.5 %collective-permute-start.41 = (f32[4,10,18,1]{3,0,2,1:T(4,128)S(1)}, f32[4,10,18,1]{3,0,2,1:T(4,128)S(1)}, u32[]{:S(2)}, u32[]{:S(2)}) collective-permute-start(f32[4,10,18,1]{3,0,2,1:T(4,128)S(1)} %get-tuple-element.113), channel_id=1, source_target_pairs={{0,1},{1,2},{2,3},{4,5},{5,6},{6,7},{8,9},{9,10},{10,11},{12,13},{... | collective-permute-start | bytes 8648 | tf_op jit(solution)/shard_map/ppermute | solution.py:19
  (25 other events, 175.3 us)
where the time goes:
time: 371 us; the launch traced here: 370 us
  blocking collectives  138 us (37%)
  starting transfers between devices  110 us (30%)
  waiting for transfers between devices  57.7 us (16%)
  other arithmetic  29.1 us (8%)
  local copies, waits for them, and re-layouts  26.4 us (7%)
  matrix products  6.55 us (2%)
    all_gather x1, blocking collectives, agglomerate(): gathered = lax.all_gather(flattened, ('gx', 'gy', 'gz'), axis=1, tiled=True)  61.1 us
    ppermute x21, starting transfers between devices, with_halo(): before = lax.ppermute(last, axis, up)  56.1 us
    ppermute x21, starting transfers between devices, with_halo(): after = lax.ppermute(leading, axis, down)  53.7 us
    psum x1, blocking collectives, per_device(): projection = lax.psum(basis_local, ('gx', 'gy', 'gz')) / total_cells  38.6 us
    psum x1, blocking collectives, per_device(): gram = lax.psum(gram_local, ('gx', 'gy', 'gz')) / total_cells  38.6 us
    ppermute x21, waiting for transfers between devices, with_halo(): after = lax.ppermute(leading, axis, down)  36.8 us
    ppermute x21, waiting for transfers between devices, with_halo(): before = lax.ppermute(last, axis, up)  20.8 us
    reduce_sum x14, other arithmetic, restrict(): field.reshape(depth, size_a // 2, 2, size_b // 2, 2, size_c // 2, 2)  13 us
  transfers between devices with their start and end apart: 42, of which 22 were waited for; matrix products, arithmetic and copies ran while one was open for 7% of the time, Pallas kernels for 0%

commit v1 on v0

--- a/solution.py
+++ b/solution.py
@@ -131,7 +131,7 @@
         local_cells * lax.axis_size("gx") * lax.axis_size("gy") * lax.axis_size("gz")
     )
     basis_local = jnp.einsum("mxyz,jxyz->mj", old_basis, previous, precision=HIGH)
-    projection = lax.psum(basis_local, ("gx", "gy", "gz")) / total_cells
+    projection = jnp.sum(lax.all_gather(basis_local, ("gx", "gy", "gz")), axis=0) / total_cells
     remainder = previous - jnp.einsum("mxyz,mj->jxyz", old_basis, projection, precision=HIGH)
     gram_local = jnp.einsum("ixyz,jxyz->ij", remainder, remainder, precision=HIGH)
     gram = lax.psum(gram_local, ("gx", "gy", "gz")) / total_cells

time: 371 us -> 395 us (1.065)
  blocking collectives: 138 us -> 157 us
  starting transfers between devices: 110 us -> 117 us
    all_gather x0 -> x1, blocking collectives: none -> 55.9 us  [per_device(): lax.all_gather(basis_local, ('gx', 'gy', 'gz'))]
    psum x1 -> x0, blocking collectives: 38.6 us -> none  [per_device(): projection = lax.psum(basis_local, ('gx', 'gy', 'gz')) / total_cells]
    ppermute x21, starting transfers between devices: 56.1 us -> 63.3 us  [with_halo(): before = lax.ppermute(last, axis, up)]
  transfers between devices with their start and end apart: 42 -> 42, of which waited for: 22 -> 22; matrix products, arithmetic and copies ran while one was open for 7% -> 6% of each run, Pallas kernels for 0% -> 0%
where the time goes in v1:
time: 395 us; the launch traced here: 394 us
  blocking collectives  157 us (40%)
  starting transfers between devices  117 us (30%)
  waiting for transfers between devices  56.6 us (14%)
  other arithmetic  28.1 us (7%)
  local copies, waits for them, and re-layouts  27.5 us (7%)
  matrix products  5.53 us (1%)
    ppermute x21, starting transfers between devices, with_halo(): before = lax.ppermute(last, axis, up)  63.3 us
    all_gather x1, blocking collectives, agglomerate(): gathered = lax.all_gather(flattened, ('gx', 'gy', 'gz'), axis=1, tiled=True)  62.2 us
    all_gather x1, blocking collectives, per_device(): lax.all_gather(basis_local, ('gx', 'gy', 'gz'))  55.9 us
    ppermute x21, starting transfers between devices, with_halo(): after = lax.ppermute(leading, axis, down)  53.6 us
    psum x1, blocking collectives, per_device(): gram = lax.psum(gram_local, ('gx', 'gy', 'gz')) / total_cells  39.1 us
    ppermute x21, waiting for transfers between devices, with_halo(): after = lax.ppermute(leading, axis, down)  36.4 us
    ppermute x21, waiting for transfers between devices, with_halo(): before = lax.ppermute(last, axis, up)  20.2 us
    reduce_sum x14, other arithmetic, restrict(): field.reshape(depth, size_a // 2, 2, size_b // 2, 2, size_c // 2, 2)  13 us
  transfers between devices with their start and end apart: 42, of which 22 were waited for; matrix products, arithmetic and copies ran while one was open for 6% of the time, Pallas kernels for 0%

profile of v1, /device:TPU:25, one launch (start us, length us, event | category | flops | bytes accessed | tf_op | source)
XLA Modules:
  0.0 393.9 jit_solution(6417869591993364343)
XLA Ops:
  1.6 3.7 collective-permute-start
  7.2 6.3 %reshape_broadcast_in_dim.3 = f32[4,2,8,2,64,2]{5,4,3,2,1,0:T(8,128)} reshape(f32[8,16,128]{2,1,0:T(8,128)} %param.15) | data formatting | bytes 131072 | tf_op jit(solution)/shard_map/reshape;broadcast_in_dim | solution.py:43
  20.6 3.6 collective-permute-done.3
  26.9 4.0 %collective-permute-start.5 = (f32[5,12,20,2]{2,3,1,0:T(2,128)S(1)}, f32[5,12,20,2]{2,3,1,0:T(2,128)S(1)}, u32[]{:S(2)}, u32[]{:S(2)}) collective-permute-start(f32[5,12,20,2]{2,3,1,0:T(2,128)S(1)} %copy.763), channel_id=1, source_target_pairs={{1,0},{2,1},{3,2},{5,4},{6,5},{7,6},{9,8},{10,9},{11,10},{13,12},{... | collective-permute-start | bytes 28808 | tf_op jit(solution)/shard_map/ppermute | solution.py:20
  32.3 55.9 %all-gather.1 = f32[32,4,4]{2,1,0:T(4,128)S(1)} all-gather(f32[1,4,4]{2,1,0:T(4,128)S(1)} %convolution_bitcast_fusion.1), channel_id=2, replica_groups=mesh['gx'=4,'gy'=2,'gz'=4] {'gx','gy','gz'}, dimensions={0}, use_global_device_ids=true | all-gather | bytes 2112 | tf_op jit(solution)/shard_map/all_gather | solution.py:134
  92.9 4.7 %copy.687 = f32[4,8,16,128]{0,3,2,1:T(8,128)} copy(f32[4,8,16,128]{3,2,1,0:T(8,128)S(1)} %fusion.35) | data formatting | bytes 524288 | tf_op jit(solution)/shard_map/sub | solution.py:112
  97.7 8.7 %reduce_sum.111 = f32[4,4,8,64]{0,3,2,1:T(8,128)S(1)} reduce(f32[4,4,2,8,2,64,2]{0,6,5,4,3,2,1:T(2,128)} %bitcast.134, f32[]{:T(128)} %constant.246.clone.1), dimensions={2,4,6}, to_apply=%region_4.0 | reduce | flops 57344 | bytes 294916 | tf_op jit(solution)/shard_map/reduce_sum | solution.py:43
  106.8 13.2 %collective-permute-start.6 = (f32[5,2,8,64]{3,2,1,0:T(8,128)S(1)}, f32[5,2,8,64]{3,2,1,0:T(8,128)S(1)}, u32[]{:S(2)}, u32[]{:S(2)}) collective-permute-start(f32[5,2,8,64]{3,2,1,0:T(8,128)S(1)} %get-tuple-element.154), channel_id=1, source_target_pairs={{0,8},{8,16},{16,24},{1,9},{9,17},{17,25},{2,10},{10,18},{18,26},{... | collective-permute-start | bytes 61448 | tf_op jit(solution)/shard_map/ppermute | solution.py:19
  132.9 4.5 %collective-permute-start.11 = (f32[5,8,12,2]{3,1,2,0:T(8,128)S(1)}, f32[5,8,12,2]{3,1,2,0:T(8,128)S(1)}, u32[]{:S(2)}, u32[]{:S(2)}) collective-permute-start(f32[5,8,12,2]{3,1,2,0:T(8,128)S(1)} %get-tuple-element.131), channel_id=1, source_target_pairs={{1,0},{2,1},{3,2},{5,4},{6,5},{7,6},{9,8},{10,9},{11,10},{13,12},{... | collective-permute-start | bytes 11528 | tf_op jit(solution)/shard_map/ppermute | solution.py:20
  149.7 39.1 %psum.7 = f32[4,4]{0,1:T(4,128)S(1)} all-reduce(f32[4,4]{0,1:T(4,128)S(1)} %convolution_bitcast_fusion), channel_id=1, replica_groups=mesh['gx'=4,'gy'=2,'gz'=4] {'gx','gy','gz'}, use_global_device_ids=true, to_apply=%region_1.0 | all-reduce | flops 16 | bytes 128 | tf_op jit(solution)/shard_map/psum | solution.py:137
  188.8 4.3 %collective-permute-start.14 = (f32[5,6,2,32]{3,2,1,0:T(2,128)S(1)}, f32[5,6,2,32]{3,2,1,0:T(2,128)S(1)}, u32[]{:S(2)}, u32[]{:S(2)}) collective-permute-start(f32[5,6,2,32]{3,2,1,0:T(2,128)S(1)} %get-tuple-element.158), channel_id=1, source_target_pairs={{0,4},{1,5},{2,6},{3,7},{8,12},{9,13},{10,14},{11,15},{16,20},{17,... | collective-permute-start | bytes 23048 | tf_op jit(solution)/shard_map/ppermute | solution.py:19
  199.2 4.3 %collective-permute-start.17 = (f32[5,6,8,2]{3,2,1,0:T(8,128)S(1)}, f32[5,6,8,2]{3,2,1,0:T(8,128)S(1)}, u32[]{:S(2)}, u32[]{:S(2)}) collective-permute-start(f32[5,6,8,2]{3,2,1,0:T(8,128)S(1)} %get-tuple-element.151), channel_id=1, source_target_pairs={{1,0},{2,1},{3,2},{5,4},{6,5},{7,6},{9,8},{10,9},{11,10},{13,12},{... | collective-permute-start | bytes 5768 | tf_op jit(solution)/shard_map/ppermute | solution.py:20
  206.3 62.2 %all-gather.2 = f32[32,32,5]{1,2,0:T(8,128)S(1)} all-gather(f32[1,32,5]{1,2,0:T(8,128)S(1)} %maximum_bitcast_fusion), channel_id=1, replica_groups=mesh['gx'=4,'gy'=2,'gz'=4] {'gx','gy','gz'}, dimensions={0}, use_global_device_ids=true | all-gather | bytes 21120 | tf_op jit(solution)/shard_map/all_gather | solution.py:74
  272.9 8.6 %collective-permute-start.18 = (f32[4,1,4,32]{3,2,1,0:T(4,128)S(1)}, f32[4,1,4,32]{3,2,1,0:T(4,128)S(1)}, u32[]{:S(2)}, u32[]{:S(2)}) collective-permute-start(f32[4,1,4,32]{3,2,1,0:T(4,128)S(1)} %get-tuple-element.175), channel_id=1, source_target_pairs={{8,0},{16,8},{24,16},{9,1},{17,9},{25,17},{10,2},{18,10},{26,18},{... | collective-permute-start | bytes 6152 | tf_op jit(solution)/shard_map/ppermute | solution.py:20
  297.2 4.0 %collective-permute-done.23 = f32[4,4,6,1]{3,1,2,0:T(4,128)S(1)} collective-permute-done((f32[4,4,6,1]{3,1,2,0:T(4,128)S(1)}, f32[4,4,6,1]{3,1,2,0:T(4,128)S(1)}, u32[]{:S(2)}, u32[]{:S(2)}) %collective-permute-start.23) | collective-permute-done | bytes 416 | tf_op jit(solution)/shard_map/ppermute | solution.py:19
  305.2 5.3 %collective-permute-start.25 = (f32[4,1,8,64]{3,2,1,0:T(8,128)S(1)}, f32[4,1,8,64]{3,2,1,0:T(8,128)S(1)}, u32[]{:S(2)}, u32[]{:S(2)}) collective-permute-start(f32[4,1,8,64]{3,2,1,0:T(8,128)S(1)} %get-tuple-element.156), channel_id=1, source_target_pairs={{0,8},{8,16},{16,24},{1,9},{9,17},{17,25},{2,10},{10,18},{18,26},{... | collective-permute-start | bytes 24584 | tf_op jit(solution)/shard_map/ppermute | solution.py:19
  317.9 3.6 collective-permute-start.28
  323.7 4.1 %collective-permute-done.29 = f32[4,6,10,1]{3,0,2,1:T(4,128)S(1)} collective-permute-done((f32[4,6,10,1]{3,0,2,1:T(4,128)S(1)}, f32[4,6,10,1]{3,0,2,1:T(4,128)S(1)}, u32[]{:S(2)}, u32[]{:S(2)}) %collective-permute-start.29) | collective-permute-done | bytes 992 | tf_op jit(solution)/shard_map/ppermute | solution.py:19
  335.2 6.5 %collective-permute-start.31 = (f32[4,1,16,128]{3,2,1,0:T(8,128)S(1)}, f32[4,1,16,128]{3,2,1,0:T(8,128)S(1)}, u32[]{:S(2)}, u32[]{:S(2)}) collective-permute-start(f32[4,1,16,128]{3,2,1,0:T(8,128)S(1)} %get-tuple-element.128), channel_id=1, source_target_pairs={{0,8},{8,16},{16,24},{1,9},{9,17},{17,25},{2,10},{10,18},{18,26},{... | collective-permute-start | bytes 98312 | tf_op jit(solution)/shard_map/ppermute | solution.py:19
  355.6 3.8 collective-permute-done.34
  359.4 4.1 %collective-permute-done.35 = f32[4,10,18,1]{3,0,2,1:T(4,128)S(1)} collective-permute-done((f32[4,10,18,1]{3,0,2,1:T(4,128)S(1)}, f32[4,10,18,1]{3,0,2,1:T(4,128)S(1)}, u32[]{:S(2)}, u32[]{:S(2)}) %collective-permute-start.35) | collective-permute-done | bytes 2912 | tf_op jit(solution)/shard_map/ppermute | solution.py:19
  366.1 4.1 %collective-permute-start.37 = (f32[4,1,16,128]{3,2,1,0:T(8,128)S(1)}, f32[4,1,16,128]{3,2,1,0:T(8,128)S(1)}, u32[]{:S(2)}, u32[]{:S(2)}) collective-permute-start(f32[4,1,16,128]{3,2,1,0:T(8,128)S(1)} %get-tuple-element.126), channel_id=1, source_target_pairs={{0,8},{8,16},{16,24},{1,9},{9,17},{17,25},{2,10},{10,18},{18,26},{... | collective-permute-start | bytes 98312 | tf_op jit(solution)/shard_map/ppermute | solution.py:19
  383.5 4.7 %collective-permute-done.40 = f32[4,10,18,1]{3,0,2,1:T(4,128)S(1)} collective-permute-done((f32[4,10,18,1]{3,0,2,1:T(4,128)S(1)}, f32[4,10,18,1]{3,0,2,1:T(4,128)S(1)}, u32[]{:S(2)}, u32[]{:S(2)}) %collective-permute-start.40) | collective-permute-done | bytes 2912 | tf_op jit(solution)/shard_map/ppermute | solution.py:20
  388.2 4.4 %collective-permute-done.41 = f32[4,10,18,1]{3,0,2,1:T(4,128)S(1)} collective-permute-done((f32[4,10,18,1]{3,0,2,1:T(4,128)S(1)}, f32[4,10,18,1]{3,0,2,1:T(4,128)S(1)}, u32[]{:S(2)}, u32[]{:S(2)}) %collective-permute-start.41) | collective-permute-done | bytes 2912 | tf_op jit(solution)/shard_map/ppermute | solution.py:19
  (281 shorter events, 124.1 us)
Async XLA Ops:
  1.6 14.5 %collective-permute-start = (f32[5,2,16,128]{3,2,1,0:T(8,128)S(1)}, f32[5,2,16,128]{3,2,1,0:T(8,128)S(1)}, u32[]{:S(2)}, u32[]{:S(2)}) collective-permute-start(f32[5,2,16,128]{3,2,1,0:T(8,128)S(1)} %get-tuple-element.122), channel_id=1, source_target_pairs={{0,8},{8,16},{16,24},{1,9},{9,17},{17,25},{2,10},{10,18},{18,26},{... | collective-permute-start | bytes 245768 | tf_op jit(solution)/shard_map/ppermute | solution.py:19
  5.3 10.8 %collective-permute-start.1 = (f32[5,2,16,128]{3,2,1,0:T(8,128)S(1)}, f32[5,2,16,128]{3,2,1,0:T(8,128)S(1)}, u32[]{:S(2)}, u32[]{:S(2)}) collective-permute-start(f32[5,2,16,128]{3,2,1,0:T(8,128)S(1)} %get-tuple-element.123), channel_id=1, source_target_pairs={{8,0},{16,8},{24,16},{9,1},{17,9},{25,17},{10,2},{18,10},{26,18},{... | collective-permute-start | bytes 245768 | tf_op jit(solution)/shard_map/ppermute | solution.py:20
  25.1 63.3 %collective-permute-start.4 = (f32[5,12,20,2]{2,3,1,0:T(2,128)S(1)}, f32[5,12,20,2]{2,3,1,0:T(2,128)S(1)}, u32[]{:S(2)}, u32[]{:S(2)}) collective-permute-start(f32[5,12,20,2]{2,3,1,0:T(2,128)S(1)} %copy.762), channel_id=1, source_target_pairs={{0,1},{1,2},{2,3},{4,5},{5,6},{6,7},{8,9},{9,10},{10,11},{12,13},{... | collective-permute-start | bytes 28808 | tf_op jit(solution)/shard_map/ppermute | solution.py:19
  26.9 62.0 %collective-permute-start.5 = (f32[5,12,20,2]{2,3,1,0:T(2,128)S(1)}, f32[5,12,20,2]{2,3,1,0:T(2,128)S(1)}, u32[]{:S(2)}, u32[]{:S(2)}) collective-permute-start(f32[5,12,20,2]{2,3,1,0:T(2,128)S(1)} %copy.763), channel_id=1, source_target_pairs={{1,0},{2,1},{3,2},{5,4},{6,5},{7,6},{9,8},{10,9},{11,10},{13,12},{... | collective-permute-start | bytes 28808 | tf_op jit(solution)/shard_map/ppermute | solution.py:20
  106.8 16.6 %collective-permute-start.6 = (f32[5,2,8,64]{3,2,1,0:T(8,128)S(1)}, f32[5,2,8,64]{3,2,1,0:T(8,128)S(1)}, u32[]{:S(2)}, u32[]{:S(2)}) collective-permute-start(f32[5,2,8,64]{3,2,1,0:T(8,128)S(1)} %get-tuple-element.154), channel_id=1, source_target_pairs={{0,8},{8,16},{16,24},{1,9},{9,17},{17,25},{2,10},{10,18},{18,26},{... | collective-permute-start | bytes 61448 | tf_op jit(solution)/shard_map/ppermute | solution.py:19
  131.6 9.5 %collective-permute-start.10 = (f32[5,8,12,2]{3,1,2,0:T(8,128)S(1)}, f32[5,8,12,2]{3,1,2,0:T(8,128)S(1)}, u32[]{:S(2)}, u32[]{:S(2)}) collective-permute-start(f32[5,8,12,2]{3,1,2,0:T(8,128)S(1)} %get-tuple-element.130), channel_id=1, source_target_pairs={{0,1},{1,2},{2,3},{4,5},{5,6},{6,7},{8,9},{9,10},{10,11},{12,13},{... | collective-permute-start | bytes 11528 | tf_op jit(solution)/shard_map/ppermute | solution.py:19
  132.9 10.0 %collective-permute-start.11 = (f32[5,8,12,2]{3,1,2,0:T(8,128)S(1)}, f32[5,8,12,2]{3,1,2,0:T(8,128)S(1)}, u32[]{:S(2)}, u32[]{:S(2)}) collective-permute-start(f32[5,8,12,2]{3,1,2,0:T(8,128)S(1)} %get-tuple-element.131), channel_id=1, source_target_pairs={{1,0},{2,1},{3,2},{5,4},{6,5},{7,6},{9,8},{10,9},{11,10},{13,12},{... | collective-permute-start | bytes 11528 | tf_op jit(solution)/shard_map/ppermute | solution.py:20
  145.3 43.4 %collective-permute-start.12 = (f32[5,2,4,32]{3,2,1,0:T(4,128)S(1)}, f32[5,2,4,32]{3,2,1,0:T(4,128)S(1)}, u32[]{:S(2)}, u32[]{:S(2)}) collective-permute-start(f32[5,2,4,32]{3,2,1,0:T(4,128)S(1)} %pad_maximum_fusion.50), channel_id=1, source_target_pairs={{0,8},{8,16},{16,24},{1,9},{9,17},{17,25},{2,10},{10,18},{18,26},{... | collective-permute-start | bytes 15368 | tf_op jit(solution)/shard_map/ppermute | solution.py:19
  147.3 41.5 %collective-permute-start.13 = (f32[5,2,4,32]{3,2,1,0:T(4,128)S(1)}, f32[5,2,4,32]{3,2,1,0:T(4,128)S(1)}, u32[]{:S(2)}, u32[]{:S(2)}) collective-permute-start(f32[5,2,4,32]{3,2,1,0:T(4,128)S(1)} %pad_maximum_fusion.50), channel_id=1, source_target_pairs={{8,0},{16,8},{24,16},{9,1},{17,9},{25,17},{10,2},{18,10},{26,18},{... | collective-permute-start | bytes 15368 | tf_op jit(solution)/shard_map/ppermute | solution.py:20
  188.8 5.8 %collective-permute-start.14 = (f32[5,6,2,32]{3,2,1,0:T(2,128)S(1)}, f32[5,6,2,32]{3,2,1,0:T(2,128)S(1)}, u32[]{:S(2)}, u32[]{:S(2)}) collective-permute-start(f32[5,6,2,32]{3,2,1,0:T(2,128)S(1)} %get-tuple-element.158), channel_id=1, source_target_pairs={{0,4},{1,5},{2,6},{3,7},{8,12},{9,13},{10,14},{11,15},{16,20},{17,... | collective-permute-start | bytes 23048 | tf_op jit(solution)/shard_map/ppermute | solution.py:19
  197.9 6.0 %collective-permute-start.16 = (f32[5,6,8,2]{3,2,1,0:T(8,128)S(1)}, f32[5,6,8,2]{3,2,1,0:T(8,128)S(1)}, u32[]{:S(2)}, u32[]{:S(2)}) collective-permute-start(f32[5,6,8,2]{3,2,1,0:T(8,128)S(1)} %get-tuple-element.150), channel_id=1, source_target_pairs={{0,1},{1,2},{2,3},{4,5},{5,6},{6,7},{8,9},{9,10},{10,11},{12,13},{... | collective-permute-start | bytes 5768 | tf_op jit(solution)/shard_map/ppermute | solution.py:19
  199.2 6.2 %collective-permute-start.17 = (f32[5,6,8,2]{3,2,1,0:T(8,128)S(1)}, f32[5,6,8,2]{3,2,1,0:T(8,128)S(1)}, u32[]{:S(2)}, u32[]{:S(2)}) collective-permute-start(f32[5,6,8,2]{3,2,1,0:T(8,128)S(1)} %get-tuple-element.151), channel_id=1, source_target_pairs={{1,0},{2,1},{3,2},{5,4},{6,5},{7,6},{9,8},{10,9},{11,10},{13,12},{... | collective-permute-start | bytes 5768 | tf_op jit(solution)/shard_map/ppermute | solution.py:20
  272.9 12.5 %collective-permute-start.18 = (f32[4,1,4,32]{3,2,1,0:T(4,128)S(1)}, f32[4,1,4,32]{3,2,1,0:T(4,128)S(1)}, u32[]{:S(2)}, u32[]{:S(2)}) collective-permute-start(f32[4,1,4,32]{3,2,1,0:T(4,128)S(1)} %get-tuple-element.175), channel_id=1, source_target_pairs={{8,0},{16,8},{24,16},{9,1},{17,9},{25,17},{10,2},{18,10},{26,18},{... | collective-permute-start | bytes 6152 | tf_op jit(solution)/shard_map/ppermute | solution.py:20
  295.3 5.9 %collective-permute-start.23 = (f32[4,4,6,1]{3,1,2,0:T(4,128)S(1)}, f32[4,4,6,1]{3,1,2,0:T(4,128)S(1)}, u32[]{:S(2)}, u32[]{:S(2)}) collective-permute-start(f32[4,4,6,1]{3,1,2,0:T(4,128)S(1)} %get-tuple-element.163), channel_id=1, source_target_pairs={{0,1},{1,2},{2,3},{4,5},{5,6},{6,7},{8,9},{9,10},{10,11},{12,13},{... | collective-permute-start | bytes 1160 | tf_op jit(solution)/shard_map/ppermute | solution.py:19
  302.0 9.1 %collective-permute-start.24 = (f32[4,1,8,64]{3,2,1,0:T(8,128)S(1)}, f32[4,1,8,64]{3,2,1,0:T(8,128)S(1)}, u32[]{:S(2)}, u32[]{:S(2)}) collective-permute-start(f32[4,1,8,64]{3,2,1,0:T(8,128)S(1)} %get-tuple-element.157), channel_id=1, source_target_pairs={{8,0},{16,8},{24,16},{9,1},{17,9},{25,17},{10,2},{18,10},{26,18},{... | collective-permute-start | bytes 24584 | tf_op jit(solution)/shard_map/ppermute | solution.py:20
  305.2 6.1 %collective-permute-start.25 = (f32[4,1,8,64]{3,2,1,0:T(8,128)S(1)}, f32[4,1,8,64]{3,2,1,0:T(8,128)S(1)}, u32[]{:S(2)}, u32[]{:S(2)}) collective-permute-start(f32[4,1,8,64]{3,2,1,0:T(8,128)S(1)} %get-tuple-element.156), channel_id=1, source_target_pairs={{0,8},{8,16},{16,24},{1,9},{9,17},{17,25},{2,10},{10,18},{18,26},{... | collective-permute-start | bytes 24584 | tf_op jit(solution)/shard_map/ppermute | solution.py:19
  321.6 6.2 %collective-permute-start.29 = (f32[4,6,10,1]{3,0,2,1:T(4,128)S(1)}, f32[4,6,10,1]{3,0,2,1:T(4,128)S(1)}, u32[]{:S(2)}, u32[]{:S(2)}) collective-permute-start(f32[4,6,10,1]{3,0,2,1:T(4,128)S(1)} %get-tuple-element.147), channel_id=1, source_target_pairs={{0,1},{1,2},{2,3},{4,5},{5,6},{6,7},{8,9},{9,10},{10,11},{12,13},{... | collective-permute-start | bytes 2888 | tf_op jit(solution)/shard_map/ppermute | solution.py:19
  333.3 10.3 %collective-permute-start.30 = (f32[4,1,16,128]{3,2,1,0:T(8,128)S(1)}, f32[4,1,16,128]{3,2,1,0:T(8,128)S(1)}, u32[]{:S(2)}, u32[]{:S(2)}) collective-permute-start(f32[4,1,16,128]{3,2,1,0:T(8,128)S(1)} %get-tuple-element.129), channel_id=1, source_target_pairs={{8,0},{16,8},{24,16},{9,1},{17,9},{25,17},{10,2},{18,10},{26,18},{... | collective-permute-start | bytes 98312 | tf_op jit(solution)/shard_map/ppermute | solution.py:20
  335.2 8.4 %collective-permute-start.31 = (f32[4,1,16,128]{3,2,1,0:T(8,128)S(1)}, f32[4,1,16,128]{3,2,1,0:T(8,128)S(1)}, u32[]{:S(2)}, u32[]{:S(2)}) collective-permute-start(f32[4,1,16,128]{3,2,1,0:T(8,128)S(1)} %get-tuple-element.128), channel_id=1, source_target_pairs={{0,8},{8,16},{16,24},{1,9},{9,17},{17,25},{2,10},{10,18},{18,26},{... | collective-permute-start | bytes 98312 | tf_op jit(solution)/shard_map/ppermute | solution.py:19
  350.7 8.6 %collective-permute-start.34 = (f32[4,10,18,1]{3,0,2,1:T(4,128)S(1)}, f32[4,10,18,1]{3,0,2,1:T(4,128)S(1)}, u32[]{:S(2)}, u32[]{:S(2)}) collective-permute-start(f32[4,10,18,1]{3,0,2,1:T(4,128)S(1)} %get-tuple-element.116), channel_id=1, source_target_pairs={{1,0},{2,1},{3,2},{5,4},{6,5},{7,6},{9,8},{10,9},{11,10},{13,12},{... | collective-permute-start | bytes 8648 | tf_op jit(solution)/shard_map/ppermute | solution.py:20
  353.2 10.3 %collective-permute-start.35 = (f32[4,10,18,1]{3,0,2,1:T(4,128)S(1)}, f32[4,10,18,1]{3,0,2,1:T(4,128)S(1)}, u32[]{:S(2)}, u32[]{:S(2)}) collective-permute-start(f32[4,10,18,1]{3,0,2,1:T(4,128)S(1)} %get-tuple-element.117), channel_id=1, source_target_pairs={{0,1},{1,2},{2,3},{4,5},{5,6},{6,7},{8,9},{9,10},{10,11},{12,13},{... | collective-permute-start | bytes 8648 | tf_op jit(solution)/shard_map/ppermute | solution.py:19
  364.2 6.6 %collective-permute-start.36 = (f32[4,1,16,128]{3,2,1,0:T(8,128)S(1)}, f32[4,1,16,128]{3,2,1,0:T(8,128)S(1)}, u32[]{:S(2)}, u32[]{:S(2)}) collective-permute-start(f32[4,1,16,128]{3,2,1,0:T(8,128)S(1)} %get-tuple-element.127), channel_id=1, source_target_pairs={{8,0},{16,8},{24,16},{9,1},{17,9},{25,17},{10,2},{18,10},{26,18},{... | collective-permute-start | bytes 98312 | tf_op jit(solution)/shard_map/ppermute | solution.py:20
  378.2 10.0 %collective-permute-start.40 = (f32[4,10,18,1]{3,0,2,1:T(4,128)S(1)}, f32[4,10,18,1]{3,0,2,1:T(4,128)S(1)}, u32[]{:S(2)}, u32[]{:S(2)}) collective-permute-start(f32[4,10,18,1]{3,0,2,1:T(4,128)S(1)} %get-tuple-element.112), channel_id=1, source_target_pairs={{1,0},{2,1},{3,2},{5,4},{6,5},{7,6},{9,8},{10,9},{11,10},{13,12},{... | collective-permute-start | bytes 8648 | tf_op jit(solution)/shard_map/ppermute | solution.py:20
  380.1 12.5 %collective-permute-start.41 = (f32[4,10,18,1]{3,0,2,1:T(4,128)S(1)}, f32[4,10,18,1]{3,0,2,1:T(4,128)S(1)}, u32[]{:S(2)}, u32[]{:S(2)}) collective-permute-start(f32[4,10,18,1]{3,0,2,1:T(4,128)S(1)} %get-tuple-element.113), channel_id=1, source_target_pairs={{0,1},{1,2},{2,3},{4,5},{5,6},{6,7},{8,9},{9,10},{10,11},{12,13},{... | collective-permute-start | bytes 8648 | tf_op jit(solution)/shard_map/ppermute | solution.py:19
  (25 other events, 154.3 us)
